TPU v7x, 32 devices: a whole 2x2x4 slice. The times are simulated.
32 devices in a mesh: dp: 4 (over y, core), seq: 8 (over z, x).
Axes of the slice: x: 2, y: 2, z: 4, core: 2. Of those that a mesh axis runs over, the one named last changes fastest.
Arguments:
- tokens: bfloat16 [32768, 2048], P(('dp', 'seq')), parts along dimension 0, may hold values from -6 to 6
- chosen: int32 [4096], P('dp'), parts along dimension 0, may hold values from 0 to 8191, as said below
- gates: float32 [4096], P('dp'), parts along dimension 0, may hold values from 0.5 to 2
- w_query: bfloat16 [2048, 1024], P('seq'), may hold values from -1.8561553 to 1.8561553
- w_key: bfloat16 [2048, 256], P('seq'), may hold values from -0.088388348 to 0.088388348
- w_value: bfloat16 [2048, 256], P('seq'), may hold values from -0.125 to 0.125
- w_out: bfloat16 [1024, 2048], P(None, 'seq'), may hold values from -0.5 to 0.5
Outputs:
- mixed: bfloat16 [32768, 2048], P(('dp', 'seq')), parts along dimension 0
There are 4 independent parts, one for each index of `dp`. A program takes and returns all parts, laid end to end along the dimension named above; an argument that names none is the same for every part. Nothing has to cross between parts.
Inputs may be any that keep to these rules, and one draw needn't show every extreme that they name: `chosen`: distinct positions in increasing order; at most 256 of them lie in one device's 1024 consecutive positions, and exactly 256 lie in some device's positions.
All inputs are finite; a program needn't handle non-finite values.
Results may differ from a plain program's by a relative error of at most 0.006.
Values may be sent and summed in bfloat16 or wider, within the bound.
A program may use at most 128 MiB of HBM per device.

v0:
```python
import math
import jax
import jax.numpy as jnp
from jax import lax
from jax.sharding import PartitionSpec as P

HEADS = 8
KV_HEADS = 2
HEAD_DIM = 128
ROWS_DEV = 128
MOST_OWN = 256
neg_fill = -1e30


def normalize(row_block):
    widened = row_block.astype(jnp.float32)
    scale_rows = lax.rsqrt(jnp.mean(widened * widened, axis=1, keepdims=True) + 1e-06)
    return (widened * scale_rows).astype(jnp.bfloat16)


def per_device(tokens, chosen, gates, w_query, w_key, w_value, w_out):
    shards = lax.axis_size("seq")
    my_index = lax.axis_index("seq")
    tok_rows = tokens.shape[0]
    model_width = tokens.shape[1]
    picked_total = chosen.shape[0]
    slot_count = (MOST_OWN - 1) // shards + 1
    group_size = HEADS // KV_HEADS
    owner_of = chosen // tok_rows
    owners = jnp.arange(shards, dtype=jnp.int32)
    counts = jnp.sum((owner_of[None, :] == owners[:, None]).astype(jnp.int32), axis=1)
    starts = jnp.cumsum(counts) - counts
    my_start = starts[my_index]
    my_count = counts[my_index]
    my_base = my_index * tok_rows
    own_steps = jnp.arange(MOST_OWN, dtype=jnp.int32)
    own_valid = own_steps < my_count
    slot_steps = jnp.arange(slot_count, dtype=jnp.int32)
    lead_step = (owners - my_start) % shards
    offset = lead_step[:, None] + shards * slot_steps[None, :]
    is_valid = offset < my_count
    flat_ids = jnp.clip((my_start + offset).reshape(-1), 0, picked_total - 1)
    flat_valid = is_valid.reshape(-1)
    spot_row = jnp.where(flat_valid, chosen[flat_ids] - my_base, 0)
    row_block = normalize(tokens[spot_row])
    outgoing = jnp.where(flat_valid[:, None], row_block, jnp.zeros_like(row_block)).reshape(
        shards, slot_count, model_width
    )
    arrived = lax.all_to_all(outgoing, "seq", split_axis=0, concat_axis=0, tiled=True)
    local_rows = jnp.arange(ROWS_DEV, dtype=jnp.int32)
    query_order = my_index + shards * local_rows
    source = owner_of[query_order]
    place_at = source * slot_count + (query_order - starts[source]) // shards
    normed = arrived.reshape(shards * slot_count, model_width)[place_at]

    def key_order_of(row_ids):
        return row_ids // ROWS_DEV + shards * (row_ids % ROWS_DEV)

    rows_here = normed.shape[0]
    pieces = (
        lax.all_gather(w_query, "seq", axis=0, tiled=True),
        lax.all_gather(w_key, "seq", axis=0, tiled=True),
        lax.all_gather(w_value, "seq", axis=0, tiled=True),
    )
    query_sum, key_sum, value_sum = tuple(
        (jnp.dot(normed, piece_now, preferred_element_type=jnp.float32) for piece_now in pieces)
    )
    query_matrix = (
        (query_sum * HEAD_DIM ** (-0.5))
        .astype(jnp.bfloat16)
        .reshape(rows_here, KV_HEADS, group_size, HEAD_DIM)
    )
    keys_all = key_sum.astype(jnp.bfloat16)
    values = value_sum.astype(jnp.bfloat16)
    start_state = (
        jnp.full((KV_HEADS, group_size, rows_here), neg_fill, jnp.float32),
        jnp.zeros((KV_HEADS, group_size, rows_here), jnp.float32),
        jnp.zeros((KV_HEADS, group_size, rows_here, HEAD_DIM), jnp.float32),
    )
    key_rows = lax.all_gather(keys_all, "seq", axis=0, tiled=True)
    value_rows = lax.all_gather(values, "seq", axis=0, tiled=True)
    length = key_rows.shape[0]
    block_rows = math.gcd(length, 512)

    def one_block(step_no, inner_state):
        top_score, weight, mixed_sum = inner_state
        first_row = step_no * block_rows
        key_portion = lax.dynamic_slice_in_dim(key_rows, first_row, block_rows, 0).reshape(
            block_rows, KV_HEADS, HEAD_DIM
        )
        value_piece = lax.dynamic_slice_in_dim(value_rows, first_row, block_rows, 0).reshape(
            block_rows, KV_HEADS, HEAD_DIM
        )
        key_order = key_order_of(first_row + jnp.arange(block_rows, dtype=jnp.int32))
        logit_scores = jnp.einsum(
            "qjfh,ujh->jfqu", query_matrix, key_portion, preferred_element_type=jnp.float32
        )
        allowed = key_order[None, :] <= query_order[:, None]
        logit_scores = jnp.where(allowed, logit_scores, neg_fill)
        fresh_top = jnp.maximum(top_score, jnp.max(logit_scores, axis=-1))
        weights_now = jnp.where(allowed, jnp.exp(logit_scores - fresh_top[..., None]), 0.0)
        shrink = jnp.exp(top_score - fresh_top)
        weight = weight * shrink + jnp.sum(weights_now, axis=-1)
        mixed_sum = mixed_sum * shrink[..., None] + jnp.einsum(
            "yoih,hyf->yoif",
            weights_now.astype(jnp.bfloat16),
            value_piece,
            preferred_element_type=jnp.float32,
        )
        return (fresh_top, weight, mixed_sum)

    top_score, weight, mixed_sum = lax.fori_loop(0, length // block_rows, one_block, start_state)
    attended = (
        jnp.transpose(mixed_sum / weight[..., None], (2, 0, 1, 3))
        .reshape(rows_here, HEADS * HEAD_DIM)
        .astype(jnp.bfloat16)
    )
    block_out = jnp.dot(
        attended,
        lax.all_gather(w_out, "seq", axis=1, tiled=True),
        preferred_element_type=jnp.float32,
    ).astype(jnp.bfloat16)
    own_compact = jnp.clip(my_start + own_steps, 0, picked_total - 1)
    slot_steps = jnp.arange(slot_count, dtype=jnp.int32)
    lead_back = (my_index - starts) % shards
    offset_back = lead_back[:, None] + shards * slot_steps[None, :]
    valid_back = offset_back < counts[:, None]
    local_k = jnp.clip((starts[:, None] + offset_back - my_index) // shards, 0, ROWS_DEV - 1)
    outgoing_back = jnp.where(
        valid_back[..., None], block_out[local_k], jnp.zeros((), jnp.bfloat16)
    )
    returned = lax.all_to_all(outgoing_back, "seq", split_axis=0, concat_axis=0, tiled=True)
    pick_at = (my_start + own_steps) % shards * slot_count + jnp.clip(
        own_steps // shards, 0, slot_count - 1
    )
    delta_rows = returned.reshape(shards * slot_count, model_width)[pick_at]
    spot_row = jnp.where(own_valid, chosen[own_compact] - my_base, tok_rows)
    lift_rows = gates[own_compact][:, None] * delta_rows.astype(jnp.float32)
    mixed = tokens.astype(jnp.float32).at[spot_row].add(lift_rows, mode="drop")
    return mixed.astype(jnp.bfloat16)


def solution(mesh):
    return jax.shard_map(
        per_device,
        mesh=mesh,
        in_specs=(
            P(("dp", "seq"), None),
            P("dp"),
            P("dp"),
            P("seq", None),
            P("seq", None),
            P("seq", None),
            P(None, "seq"),
        ),
        out_specs=P(("dp", "seq"), None),
        check_vma=False,
    )
```

profile of v0, /device:TPU:0, one launch (start us, length us, event | category | flops | bytes accessed | tf_op | source)
XLA Modules:
  0.0 318.1 jit_solution(3164678104505626016)
XLA Ops:
  13.8 1.4 gather_fusion.2
  15.3 5.1 %gather_fusion.3 = bf16[256,2048]{1,0:T(8,128)(2,1)S(1)} fusion(bf16[1024,2048]{1,0:T(8,128)(2,1)} %param.9, s32[1024]{0:T(1024)S(1)} %pad_clamp_fusion.4), kind=kCustom, calls=%fused_computation.3 | custom fusion | bytes 2098176 | tf_op jit(solution)/shard_map/gather | solution.py:45
  20.7 1.3 fusion.21
  22.0 7.3 %all-to-all-start = ((bf16[8,32,2048]{2,1,0:T(8,128)(2,1)}), bf16[8,32,2048]{2,1,0:T(8,128)(2,1)S(1)}, u32[]{:S(2)}, u32[]{:S(2)}) async-start(bf16[8,32,2048]{2,1,0:T(8,128)(2,1)} %fusion.21), calls=%async_computation | async-start | bytes 2097152 | tf_op jit(solution)/shard_map/all_to_all | solution.py:49
  30.5 4.9 %fusion.40 = s32[128]{0:T(128)S(1)} fusion(s32[128]{0:T(128)S(1)} %gather_fusion.4, s32[]{:T(128)} %bitcast.16, s32[]{:T(128)} %bitcast.17, s32[]{:T(128)} %bitcast.18, s32[]{:T(128)} %bitcast.19, s32[]{:T(128)} %bitcast.20, s32[]{:T(128)} %bitcast.22, s32[]{:T(128)} %bitcast.21, s32[]{:T(128)} %bitcast.15, s32[]{:T(128)} %axis_index.12), kind=kLoop, calls=%fused_computation.132 | loop fusion | flops 5120 | bytes 1060 | tf_op jit(solution)/shard_map/select_n | solution.py:54
  35.5 28.1 %all-to-all-done = bf16[8,32,2048]{2,1,0:T(8,128)(2,1)S(1)} async-done(((bf16[8,32,2048]{2,1,0:T(8,128)(2,1)}), bf16[8,32,2048]{2,1,0:T(8,128)(2,1)S(1)}, u32[]{:S(2)}, u32[]{:S(2)}) %all-to-all-start) | async-done | bytes 1048608 | tf_op jit(solution)/shard_map/all_to_all | solution.py:49
  64.5 1.5 convolution_convert_fusion.1
  66.1 32.1 %all_gather.22 = bf16[1024,256]{1,0:T(8,128)(2,1)S(1)} all-gather(bf16[128,256]{1,0:T(8,128)(2,1)S(1)} %convolution_convert_fusion.1), channel_id=1, replica_groups=mesh['dp'=4,'seq'=8] {'seq'}, dimensions={0}, use_global_device_ids=true | all-gather | bytes 589824 | tf_op jit(solution)/shard_map/all_gather | solution.py:81
  98.2 7.5 %all-gather.5.cloned.1.call-done = bf16[2048,256]{1,0:T(8,128)(2,1)} async-done(((bf16[256,256]{1,0:T(8,128)(2,1)}), bf16[2048,256]{1,0:T(8,128)(2,1)}) %all-gather.5.cloned.1.call-update) | async-done | bytes 1048592 | tf_op jit(solution)/shard_map/all_gather | solution.py:62
  105.7 1.5 convolution_convert_fusion.2
  107.2 33.2 %all_gather.19 = bf16[1024,256]{1,0:T(8,128)(2,1)S(1)} all-gather(bf16[128,256]{1,0:T(8,128)(2,1)S(1)} %convolution_convert_fusion.2), channel_id=1, replica_groups=mesh['dp'=4,'seq'=8] {'seq'}, dimensions={0}, use_global_device_ids=true | all-gather | bytes 589824 | tf_op jit(solution)/shard_map/all_gather | solution.py:80
  140.4 42.1 %all-gather.7.cloned.1.call-done = bf16[2048,1024]{1,0:T(8,128)(2,1)} async-done(((bf16[256,1024]{1,0:T(8,128)(2,1)}), bf16[2048,1024]{1,0:T(8,128)(2,1)}) %all-gather.7.cloned.1.call-update) | async-done | bytes 4194320 | tf_op jit(solution)/shard_map/all_gather | solution.py:61
  182.4 2.9 fusion.20
  185.6 4.9 %while.20 = (s32[]{:T(128)}, f32[2,4,128]{2,1,0:T(4,128)S(1)}, f32[2,4,128]{2,1,0:T(4,128)S(1)}, f32[2,4,128,128]{3,2,1,0:T(8,128)S(1)}, bf16[1024,256]{1,0:T(8,...) while((s32[]{:T(128)}, f32[2,4,128]{2,1,0:T(4,128)S(1)}, ...), condition=%wide.region_6.7_spmd.clone, body=%wide.region_3.6_spmd.clone.sunk | while | flops 274153728 | bytes 10556611 | solution.py:112
  190.8 66.8 %all-gather.11.cloned.1.call-done = bf16[1024,2048]{1,0:T(8,128)(2,1)} async-done(((bf16[1024,256]{1,0:T(8,128)(2,1)}), bf16[1024,2048]{1,0:T(8,128)(2,1)}) %all-gather.11.cloned.1.call-update) | async-done | bytes 4194320 | tf_op jit(solution)/shard_map/all_gather | solution.py:120
  257.5 2.9 convolution_convert_fusion
  260.5 1.4 gather_fusion.6
  262.9 3.7 %all-to-all-start.1 = ((bf16[8,32,2048]{2,1,0:T(8,128)(2,1)}), bf16[8,32,2048]{2,1,0:T(8,128)(2,1)S(1)}, u32[]{:S(2)}, u32[]{:S(2)}) async-start(bf16[8,32,2048]{2,1,0:T(8,128)(2,1)} %broadcast_select_fusion), calls=%async_computation.1 | async-start | bytes 2097152 | tf_op jit(solution)/shard_map/all_to_all | solution.py:132
  266.7 6.5 %convert_element_type.56 = f32[1024,2048]{1,0:T(8,128)} convert(bf16[1024,2048]{1,0:T(8,128)(2,1)} %param.9) | non-fusion elementwise | flops 2097152 | bytes 12582912 | tf_op jit(solution)/shard_map/convert_element_type | solution.py:139
  273.8 1.4 gather_fusion
  275.2 1.4 gather_fusion.1
  277.3 14.5 %all-to-all-done.1 = bf16[8,32,2048]{2,1,0:T(8,128)(2,1)S(1)} async-done(((bf16[8,32,2048]{2,1,0:T(8,128)(2,1)}), bf16[8,32,2048]{2,1,0:T(8,128)(2,1)S(1)}, u32[]{:S(2)}, u32[]{:S(2)}) %all-to-all-start.1) | async-done | bytes 1048608 | tf_op jit(solution)/shard_map/all_to_all | solution.py:132
  291.7 13.8 %scatter_custom_fusion = f32[1024,2048]{1,0:T(8,128)} fusion(f32[1024,2048]{1,0:T(8,128)} %convert_element_type.56, s32[256]{0:T(256)S(1)} %bitcast.130, f32[256]{0:T(256)S(1)} %gather_fusion.1, bf16[256,2048]{1,0:T(8,128)(2,1)S(1)} %bitcast.120, s32[1024]{0:T(1024)S(1)} %pad_clamp_fusion), kind=kCustom, calls=%fused_computation.43 | custom fusion | flops 1572864 | bytes 9442304 | tf_op jit(solution)/shard_map/scatter-add | solution.py:139
  305.5 6.0 %convert_element_type.70 = bf16[1024,2048]{1,0:T(8,128)(2,1)} convert(f32[1024,2048]{1,0:T(8,128)} %scatter_custom_fusion) | non-fusion elementwise | flops 2097152 | bytes 12582912 | tf_op jit(solution)/shard_map/convert_element_type | solution.py:140
  (78 shorter events, 17.3 us)
Async XLA Ops:
  6.5 268.7 %copy-start = (f32[1024]{0:T(1024)S(1)}, f32[1024]{0:T(1024)}, u32[]{:S(2)}) copy-start(f32[1024]{0:T(1024)} %param.11) | copy-start | bytes 12292
  6.5 7.3 %copy-start.1 = (s32[1024]{0:T(1024)S(1)}, s32[1024]{0:T(1024)}, u32[]{:S(2)}) copy-start(s32[1024]{0:T(1024)} %param.10) | copy-start | bytes 12292
  6.5 58.0 %all-gather.9.cloned.1.call-start = ((), (), s32[]{:S(2)}) async-start(), calls=%async_computation.4 | async-start | bytes 1179648 | tf_op jit(solution)/shard_map/all_gather | solution.py:63
  7.3 98.4 %all-gather.5.cloned.1.call-start = ((), (), s32[]{:S(2)}) async-start(), calls=%async_computation.2 | async-start | bytes 1179648 | tf_op jit(solution)/shard_map/all_gather | solution.py:62
  8.0 174.4 %all-gather.7.cloned.1.call-start = ((), (), s32[]{:S(2)}) async-start(), calls=%async_computation.3 | async-start | bytes 4718592 | tf_op jit(solution)/shard_map/all_gather | solution.py:61
  8.7 248.8 %all-gather.11.cloned.1.call-start = ((), (), s32[]{:S(2)}) async-start(), calls=%async_computation.5 | async-start | bytes 4718592 | tf_op jit(solution)/shard_map/all_gather | solution.py:120
  22.0 41.5 %all-to-all-start = ((bf16[8,32,2048]{2,1,0:T(8,128)(2,1)}), bf16[8,32,2048]{2,1,0:T(8,128)(2,1)S(1)}, u32[]{:S(2)}, u32[]{:S(2)}) async-start(bf16[8,32,2048]{2,1,0:T(8,128)(2,1)} %fusion.21), calls=%async_computation | async-start | bytes 2097152 | tf_op jit(solution)/shard_map/all_to_all | solution.py:49
  262.9 28.8 %all-to-all-start.1 = ((bf16[8,32,2048]{2,1,0:T(8,128)(2,1)}), bf16[8,32,2048]{2,1,0:T(8,128)(2,1)S(1)}, u32[]{:S(2)}, u32[]{:S(2)}) async-start(bf16[8,32,2048]{2,1,0:T(8,128)(2,1)} %broadcast_select_fusion), calls=%async_computation.1 | async-start | bytes 2097152 | tf_op jit(solution)/shard_map/all_to_all | solution.py:132
Sparse Core Ops, SparseCore 0:
  9.5 53.3 all-gather.8
  65.0 40.6 all-gather.4
  107.8 74.5 all-gather.6
  184.3 73.1 all-gather.10
where the time goes:
time: 319 us; the launch traced here: 318 us
  waiting for transfers between devices  161 us (50%)
  blocking collectives  65.3 us (20%)
  other arithmetic  39.7 us (12%)
  local copies, waits for them, and re-layouts  15.1 us (5%)
  between operations  13.4 us (4%)
  matrix products  11.8 us (4%)
  starting transfers between devices  11.1 us (3%)
    all_gather x1, waiting for transfers between devices, per_device(): lax.all_gather(w_out, 'seq', axis=1, tiled=True)  66.8 us
    all_gather x1, waiting for transfers between devices, per_device(): lax.all_gather(w_query, 'seq', axis=0, tiled=True)  42.1 us
    all_gather x1, blocking collectives, per_device(): key_rows = lax.all_gather(keys_all, 'seq', axis=0, tiled=True)  33.2 us
    all_gather x1, blocking collectives, per_device(): value_rows = lax.all_gather(values, 'seq', axis=0, tiled=True)  32.1 us
    all_to_all x1, waiting for transfers between devices, per_device(): lax.all_to_all(outgoing, 'seq', split_axis=0, concat_axis=0, tiled=True)  28.1 us
    all_to_all x1, waiting for transfers between devices, per_device(): lax.all_to_all(outgoing_back, 'seq', split_axis=0, concat_axis=0, tiled=T...  14.5 us
    scatter-add x1, other arithmetic, per_device(): mixed = tokens.astype(jnp.float32).at[spot_row].add(lift_rows, mode='drop')  13.8 us
    all_gather x1, waiting for transfers between devices, per_device(): lax.all_gather(w_key, 'seq', axis=0, tiled=True)  7.47 us
  transfers between devices with their start and end apart: 6, of which 5 were waited for; matrix products, arithmetic and copies ran while one was open for 13% of the time, Pallas kernels for 0%

commit v1 on v0

--- a/solution.py
+++ b/solution.py
@@ -77,8 +77,11 @@
         jnp.zeros((KV_HEADS, group_size, rows_here), jnp.float32),
         jnp.zeros((KV_HEADS, group_size, rows_here, HEAD_DIM), jnp.float32),
     )
-    key_rows = lax.all_gather(keys_all, "seq", axis=0, tiled=True)
-    value_rows = lax.all_gather(values, "seq", axis=0, tiled=True)
+    key_rows, value_rows = jnp.split(
+        lax.all_gather(jnp.concatenate([keys_all, values], axis=1), "seq", axis=0, tiled=True),
+        [keys_all.shape[1]],
+        axis=1,
+    )
     length = key_rows.shape[0]
     block_rows = math.gcd(length, 512)
 

time: 319 us -> 356 us (1.12)
  waiting for transfers between devices: 161 us -> 261 us
  blocking collectives: 65.3 us -> 0 us
    all_gather x2 -> x0, blocking collectives: 65.3 us -> none  [the longest x1 33.2 us: per_device(): key_rows = lax.all_gather(keys_all, 'seq', axis=0, tiled=True)]
    all_gather x0 -> x1, waiting for transfers between devices: none -> 37.8 us  [per_device(): lax.all_gather(jnp.concatenate([keys_all, values], axis=1), 'seq', axis=0...]
    all_gather x1, waiting for transfers between devices: 7.47 us -> 39.4 us  [per_device(): lax.all_gather(w_key, 'seq', axis=0, tiled=True)]
    all_gather x1, waiting for transfers between devices: 42.1 us -> 72.2 us  [per_device(): lax.all_gather(w_query, 'seq', axis=0, tiled=True)]
  transfers between devices with their start and end apart: 6 -> 7, of which waited for: 5 -> 6; matrix products, arithmetic and copies ran while one was open for 13% -> 12% of each run, Pallas kernels for 0% -> 0%
where the time goes in v1:
time: 356 us; the launch traced here: 355 us
  waiting for transfers between devices  261 us (73%)
  other arithmetic  40.4 us (11%)
  local copies, waits for them, and re-layouts  16.9 us (5%)
  between operations  13.4 us (4%)
  matrix products  11.7 us (3%)
  starting transfers between devices  11.2 us (3%)
    all_gather x1, waiting for transfers between devices, per_device(): lax.all_gather(w_query, 'seq', axis=0, tiled=True)  72.2 us
    all_gather x1, waiting for transfers between devices, per_device(): lax.all_gather(w_out, 'seq', axis=1, tiled=True)  66.8 us
    all_gather x1, waiting for transfers between devices, per_device(): lax.all_gather(w_key, 'seq', axis=0, tiled=True)  39.4 us
    all_gather x1, waiting for transfers between devices, per_device(): lax.all_gather(jnp.concatenate([keys_all, values], axis=1), 'seq', axis=0...  37.8 us
    all_to_all x1, waiting for transfers between devices, per_device(): lax.all_to_all(outgoing, 'seq', split_axis=0, concat_axis=0, tiled=True)  28.1 us
    all_to_all x1, waiting for transfers between devices, per_device(): lax.all_to_all(outgoing_back, 'seq', split_axis=0, concat_axis=0, tiled=T...  14.5 us
    scatter-add x1, other arithmetic, per_device(): mixed = tokens.astype(jnp.float32).at[spot_row].add(lift_rows, mode='drop')  13.7 us
    all_to_all x1, starting transfers between devices, per_device(): lax.all_to_all(outgoing, 'seq', split_axis=0, concat_axis=0, tiled=True)  7.28 us
  transfers between devices with their start and end apart: 7, of which 6 were waited for; matrix products, arithmetic and copies ran while one was open for 12% of the time, Pallas kernels for 0%

profile of v1, /device:TPU:0, one launch (start us, length us, event | category | flops | bytes accessed | tf_op | source)
XLA Modules:
  0.0 355.0 jit_solution(16705344098729269317)
XLA Ops:
  11.8 1.9 gather_fusion.2
  13.8 5.1 %gather_fusion.3 = bf16[256,2048]{1,0:T(8,128)(2,1)S(1)} fusion(bf16[1024,2048]{1,0:T(8,128)(2,1)} %param.9, s32[1024]{0:T(1024)S(1)} %pad_clamp_fusion.4), kind=kCustom, calls=%fused_computation.3 | custom fusion | bytes 2098176 | tf_op jit(solution)/shard_map/gather | solution.py:45
  19.2 1.3 fusion.21
  20.5 7.3 %all-to-all-start = ((bf16[8,32,2048]{2,1,0:T(8,128)(2,1)}), bf16[8,32,2048]{2,1,0:T(8,128)(2,1)S(1)}, u32[]{:S(2)}, u32[]{:S(2)}) async-start(bf16[8,32,2048]{2,1,0:T(8,128)(2,1)} %fusion.21), calls=%async_computation | async-start | bytes 2097152 | tf_op jit(solution)/shard_map/all_to_all | solution.py:49
  29.6 4.9 %fusion.40 = s32[128]{0:T(128)S(1)} fusion(s32[128]{0:T(128)S(1)} %gather_fusion.4, s32[]{:T(128)} %bitcast.16, s32[]{:T(128)} %bitcast.17, s32[]{:T(128)} %bitcast.18, s32[]{:T(128)} %bitcast.19, s32[]{:T(128)} %bitcast.20, s32[]{:T(128)} %bitcast.22, s32[]{:T(128)} %bitcast.21, s32[]{:T(128)} %bitcast.15, s32[]{:T(128)} %axis_index.12), kind=kLoop, calls=%fused_computation.133 | loop fusion | flops 5120 | bytes 1060 | tf_op jit(solution)/shard_map/select_n | solution.py:54
  34.5 28.1 %all-to-all-done = bf16[8,32,2048]{2,1,0:T(8,128)(2,1)S(1)} async-done(((bf16[8,32,2048]{2,1,0:T(8,128)(2,1)}), bf16[8,32,2048]{2,1,0:T(8,128)(2,1)S(1)}, u32[]{:S(2)}, u32[]{:S(2)}) %all-to-all-start) | async-done | bytes 1048608 | tf_op jit(solution)/shard_map/all_to_all | solution.py:49
  63.6 1.5 convolution_convert_fusion.1
  65.2 39.4 %all-gather.6.cloned.1.call-done = bf16[2048,256]{1,0:T(8,128)(2,1)} async-done(((bf16[256,256]{1,0:T(8,128)(2,1)}), bf16[2048,256]{1,0:T(8,128)(2,1)}) %all-gather.6.cloned.1.call-update) | async-done | bytes 1048592 | tf_op jit(solution)/shard_map/all_gather | solution.py:62
  104.5 1.5 convolution_convert_fusion.2
  108.1 37.8 %all-gather.10.cloned.1.call-done = bf16[1024,512]{1,0:T(8,128)(2,1)} async-done(((bf16[128,512]{1,0:T(8,128)(2,1)}), bf16[1024,512]{1,0:T(8,128)(2,1)}) %all-gather.10.cloned.1.call-update) | async-done | bytes 1048592 | tf_op jit(solution)/shard_map/all_gather | solution.py:81
  145.9 1.3 fusion.43
  147.2 72.2 %all-gather.12.cloned.1.call-done = bf16[2048,1024]{1,0:T(8,128)(2,1)} async-done(((bf16[256,1024]{1,0:T(8,128)(2,1)}), bf16[2048,1024]{1,0:T(8,128)(2,1)}) %all-gather.12.cloned.1.call-update) | async-done | bytes 4194320 | tf_op jit(solution)/shard_map/all_gather | solution.py:61
  219.4 2.9 fusion.20
  222.6 4.9 %while.20 = (s32[]{:T(128)}, f32[2,4,128]{2,1,0:T(4,128)S(1)}, f32[2,4,128]{2,1,0:T(4,128)S(1)}, f32[2,4,128,128]{3,2,1,0:T(8,128)S(1)}, bf16[1024,256]{1,0:T(8,...) while((s32[]{:T(128)}, f32[2,4,128]{2,1,0:T(4,128)S(1)}, ...), condition=%wide.region_6.7_spmd.clone, body=%wide.region_3.6_spmd.clone.sunk | while | flops 274153728 | bytes 10556611 | solution.py:115
  227.7 66.8 %all-gather.14.cloned.1.call-done = bf16[1024,2048]{1,0:T(8,128)(2,1)} async-done(((bf16[1024,256]{1,0:T(8,128)(2,1)}), bf16[1024,2048]{1,0:T(8,128)(2,1)}) %all-gather.14.cloned.1.call-update) | async-done | bytes 4194320 | tf_op jit(solution)/shard_map/all_gather | solution.py:123
  294.5 2.9 convolution_convert_fusion
  297.5 1.4 gather_fusion.6
  299.9 3.7 %all-to-all-start.1 = ((bf16[8,32,2048]{2,1,0:T(8,128)(2,1)}), bf16[8,32,2048]{2,1,0:T(8,128)(2,1)S(1)}, u32[]{:S(2)}, u32[]{:S(2)}) async-start(bf16[8,32,2048]{2,1,0:T(8,128)(2,1)} %broadcast_select_fusion), calls=%async_computation.1 | async-start | bytes 2097152 | tf_op jit(solution)/shard_map/all_to_all | solution.py:135
  303.7 6.5 %convert_element_type.56 = f32[1024,2048]{1,0:T(8,128)} convert(bf16[1024,2048]{1,0:T(8,128)(2,1)} %param.9) | non-fusion elementwise | flops 2097152 | bytes 12582912 | tf_op jit(solution)/shard_map/convert_element_type | solution.py:142
  310.9 1.4 gather_fusion
  312.2 1.4 gather_fusion.1
  314.3 14.5 %all-to-all-done.1 = bf16[8,32,2048]{2,1,0:T(8,128)(2,1)S(1)} async-done(((bf16[8,32,2048]{2,1,0:T(8,128)(2,1)}), bf16[8,32,2048]{2,1,0:T(8,128)(2,1)S(1)}, u32[]{:S(2)}, u32[]{:S(2)}) %all-to-all-start.1) | async-done | bytes 1048608 | tf_op jit(solution)/shard_map/all_to_all | solution.py:135
  328.7 13.7 %scatter_custom_fusion = f32[1024,2048]{1,0:T(8,128)} fusion(f32[1024,2048]{1,0:T(8,128)} %convert_element_type.56, s32[256]{0:T(256)S(1)} %bitcast.130, f32[256]{0:T(256)S(1)} %gather_fusion.1, bf16[256,2048]{1,0:T(8,128)(2,1)S(1)} %bitcast.120, s32[1024]{0:T(1024)S(1)} %pad_clamp_fusion), kind=kCustom, calls=%fused_computation.43 | custom fusion | flops 1572864 | bytes 9442304 | tf_op jit(solution)/shard_map/scatter-add | solution.py:142
  342.5 6.0 %convert_element_type.70 = bf16[1024,2048]{1,0:T(8,128)(2,1)} convert(f32[1024,2048]{1,0:T(8,128)} %scatter_custom_fusion) | non-fusion elementwise | flops 2097152 | bytes 12582912 | tf_op jit(solution)/shard_map/convert_element_type | solution.py:143
  (81 shorter events, 17.9 us)
Async XLA Ops:
  6.5 305.7 %copy-start = (f32[1024]{0:T(1024)S(1)}, f32[1024]{0:T(1024)}, u32[]{:S(2)}) copy-start(f32[1024]{0:T(1024)} %param.11) | copy-start | bytes 12292
  6.5 57.1 %all-gather.8.cloned.1.call-start = ((), (), s32[]{:S(2)}) async-start(), calls=%async_computation.3 | async-start | bytes 1179648 | tf_op jit(solution)/shard_map/all_gather | solution.py:63
  20.5 42.1 %all-to-all-start = ((bf16[8,32,2048]{2,1,0:T(8,128)(2,1)}), bf16[8,32,2048]{2,1,0:T(8,128)(2,1)S(1)}, u32[]{:S(2)}, u32[]{:S(2)}) async-start(bf16[8,32,2048]{2,1,0:T(8,128)(2,1)} %fusion.21), calls=%async_computation | async-start | bytes 2097152 | tf_op jit(solution)/shard_map/all_to_all | solution.py:49
  27.8 76.7 %all-gather.6.cloned.1.call-start = ((), (), s32[]{:S(2)}) async-start(), calls=%async_computation.2 | async-start | bytes 1179648 | tf_op jit(solution)/shard_map/all_gather | solution.py:62
  28.5 117.4 %all-gather.10.cloned.1.call-start = ((), (), s32[]{:S(2)}) async-start(), calls=%async_computation.4 | async-start | bytes 1179648 | tf_op jit(solution)/shard_map/all_gather | solution.py:81
  106.8 112.7 %all-gather.12.cloned.1.call-start = ((), (), s32[]{:S(2)}) async-start(), calls=%async_computation.5 | async-start | bytes 4718592 | tf_op jit(solution)/shard_map/all_gather | solution.py:61
  107.4 187.2 %all-gather.14.cloned.1.call-start = ((), (), s32[]{:S(2)}) async-start(), calls=%async_computation.6 | async-start | bytes 4718592 | tf_op jit(solution)/shard_map/all_gather | solution.py:123
  299.9 28.8 %all-to-all-start.1 = ((bf16[8,32,2048]{2,1,0:T(8,128)(2,1)}), bf16[8,32,2048]{2,1,0:T(8,128)(2,1)S(1)}, u32[]{:S(2)}, u32[]{:S(2)}) async-start(bf16[8,32,2048]{2,1,0:T(8,128)(2,1)} %broadcast_select_fusion), calls=%async_computation.1 | async-start | bytes 2097152 | tf_op jit(solution)/shard_map/all_to_all | solution.py:135
  303.7 7.2 %copy-start.1 = (s32[1024]{0:T(1024)S(1)}, s32[1024]{0:T(1024)}, u32[]{:S(2)}) copy-start(s32[1024]{0:T(1024)} %param.10) | copy-start | bytes 12292
Sparse Core Ops, SparseCore 0:
  9.5 52.9 all-gather.7
  64.6 39.8 all-gather.5
  106.9 38.9 all-gather.9
  147.9 71.4 all-gather.11
  221.3 73.1 all-gather.13
